TPU v7x, 32 devices: a whole 2x2x4 slice. The times are simulated.
32 devices in a mesh: cells: 8 (over z, x), genes: 4 (over y, core).
Axes of the slice: x: 2, y: 2, z: 4, core: 2. Of those that a mesh axis runs over, the one named last changes fastest.
Arguments:
- expression: float32 [2048, 8192], P('cells', 'genes'), may hold values from 0.1 to 3000, as said below
- donor_label: int32 [2048], P('cells'), may hold values from 0 to 255
- live_count: int32 [8], P('cells'), may hold values from 16 to 256, as said below
- genotypes: bfloat16 [4, 8, 256, 4096], P('genes', 'cells'), may hold values from 0 to 2
- covariates: float32 [256, 2], replicated, may hold values from -4 to 4
- donor_cells: int32 [256], replicated, may hold values from 200 to 4999
- win_start: int32 [4, 2048], P('genes', 'cells'), may hold values from 0 to 2048
- win_len: int32 [4, 2048], P('genes', 'cells'), may hold values from 512 to 2048, as said below
Outputs:
- correlation: float32 [4, 2048, 4096], P('genes', 'cells')
- zscore_out: float32 [4, 2048, 256], P('genes', 'cells')
Inputs may be any that keep to these rules, and one draw needn't show every extreme that they name: `live_count`: some index of cells has all 256 slots used. win_len[b0, k] is 2048 wherever k is a multiple of 256, so win_start + win_len <= 4096 throughout. `expression`: positive counts.
All inputs are finite; a program needn't handle non-finite values.
Results may differ from a plain program's by a relative error of at most 0.0003.
Values sent between devices are 32-bit elements; how exact they have to be, the bound alone decides.
A program may use at most 64 MiB of HBM per device.

v0:
```python
import jax
import jax.numpy as jnp
from jax import lax
from jax.sharding import PartitionSpec as P

HIGHEST = lax.Precision.HIGHEST
epsilon = 1e-06
cpm_scale = 10000.0


def design_matrix(covariates, donor_cells):
    log_cells = jnp.log(donor_cells.astype(jnp.float32) / 1000.0)
    ones_col = jnp.ones((covariates.shape[0], 1), jnp.float32)
    return jnp.concatenate([ones_col, log_cells[:, None], covariates], axis=1)


def invert(gram_matrix):
    width = gram_matrix.shape[0]
    augmented = jnp.concatenate([gram_matrix, jnp.eye(width, dtype=jnp.float32)], axis=1)
    for pivot in range(width):
        pivot_row = augmented[pivot] / augmented[pivot, pivot]
        augmented = augmented - augmented[:, pivot][:, None] * pivot_row[None, :]
        augmented = augmented.at[pivot].set(pivot_row)
    return augmented[:, width:]


def residualize_rows(level_rows, design, gram_inv):
    projected = jnp.dot(level_rows, design, precision=HIGHEST, preferred_element_type=jnp.float32)
    coeffs = jnp.dot(projected, gram_inv, precision=HIGHEST, preferred_element_type=jnp.float32)
    return level_rows - jnp.dot(
        coeffs, design.T, precision=HIGHEST, preferred_element_type=jnp.float32
    )


def body(
    expression, donor_label, live_count, genotypes, covariates, donor_cells, win_start, win_len
):
    donors = covariates.shape[0]
    capacity, local_genes = expression.shape
    cells_count = lax.axis_size("cells")
    block_genes = local_genes // cells_count
    design = design_matrix(covariates, donor_cells)
    gram_inv = invert(
        jnp.dot(design.T, design, precision=HIGHEST, preferred_element_type=jnp.float32)
    )
    donor_ids = jnp.arange(donors, dtype=jnp.int32)
    block_rows = min(128, capacity)
    block_count = (live_count[0] + block_rows - 1) // block_rows

    def onehot_of(labels, usable):
        return ((labels[None, :] == donor_ids[:, None]) & usable[None, :]).astype(jnp.float32)

    def local_block(turn_id):
        offset = turn_id * block_rows
        cell_rows = lax.dynamic_slice_in_dim(expression, offset, block_rows, 0)
        labels = lax.dynamic_slice_in_dim(donor_label, offset, block_rows, 0)
        usable = offset + jnp.arange(block_rows, dtype=jnp.int32) < live_count[0]
        return (cell_rows, onehot_of(labels, usable))

    def gene_major(turn_id, running):
        cell_rows, onehot = local_block(turn_id)
        return running + lax.dot_general(
            cell_rows,
            onehot,
            (((0,), (1,)), ((), ())),
            precision=HIGHEST,
            preferred_element_type=jnp.float32,
        )

    partial_value = lax.fori_loop(
        0, block_count, gene_major, jnp.zeros((local_genes, donors), jnp.float32)
    )
    totals = lax.psum(jnp.sum(partial_value, axis=0), ("cells", "genes"))
    pieces = lax.all_to_all(partial_value, "cells", split_axis=0, concat_axis=0, tiled=True)
    sums_rows = jnp.sum(pieces.reshape(cells_count, block_genes, donors), axis=0)
    level_rows = jnp.log1p(cpm_scale * sums_rows / (totals[None, :] + 1.0))
    level_rows = residualize_rows(level_rows, design, gram_inv)
    zscore_rows = level_rows * lax.rsqrt(
        jnp.mean(level_rows * level_rows, axis=1, keepdims=True) + epsilon
    )
    dosage = genotypes[0, 0].astype(jnp.float32)
    coef_x = jnp.dot(
        gram_inv,
        jnp.dot(design.T, dosage, precision=HIGHEST, preferred_element_type=jnp.float32),
        precision=HIGHEST,
        preferred_element_type=jnp.float32,
    )
    dosage_res = dosage - jnp.dot(
        design, coef_x, precision=HIGHEST, preferred_element_type=jnp.float32
    )
    dosage_z = dosage_res * lax.rsqrt(
        jnp.mean(dosage_res * dosage_res, axis=0, keepdims=True) + epsilon
    )
    correlation = (
        jnp.dot(zscore_rows, dosage_z, precision=HIGHEST, preferred_element_type=jnp.float32)
        / donors
    )
    variant = jnp.arange(dosage.shape[1], dtype=jnp.int32)
    first = win_start[0]
    inside = (variant[None, :] >= first[:, None]) & (
        variant[None, :] < (first + win_len[0])[:, None]
    )
    correlation = jnp.where(inside, correlation, jnp.float32(0.0))
    return (correlation[None], zscore_rows[None])


def solution(mesh):
    placed = (
        P("cells", "genes"),
        P("cells"),
        P("cells"),
        P("genes", "cells", None, None),
        P(),
        P(),
        P("genes", "cells"),
        P("genes", "cells"),
    )
    return jax.shard_map(
        body,
        mesh=mesh,
        in_specs=placed,
        out_specs=(P("genes", "cells", None), P("genes", "cells", None)),
        check_vma=False,
    )
```

profile of v0, /device:TPU:0, one launch (start us, length us, event | category | flops | bytes accessed | tf_op | source)
XLA Modules:
  0.0 109.5 jit_solution(6040645947162707037)
XLA Ops:
  1.3 1.5 %broadcast_in_dim.16 = f32[2048,256]{1,0:T(8,128)} broadcast(f32[]{:T(128)} %constant.148.clone.1), dimensions={} | broadcast | bytes 2097156 | tf_op jit(solution)/shard_map/broadcast_in_dim | solution.py:71
  2.8 11.4 %while.15 = (s32[]{:T(128)}, f32[2048,256]{1,0:T(8,128)}, s32[]{:T(128)}, f32[256,2048]{1,0:T(8,128)}, s32[256]{0:T(256)}, /*index=5*/s32[1]{0:T(128)}, s32[]{:T(128)}, s32[]{:T(128)}, s32[]{:T(128)}, s32[]{:T(128)}) while((s32[]{:T(128)}, f32[2048,256]{1,0:T(8,128)}, s32[]{:T(128)}, f32[256,2048]{1,0:T(8,128)}, s32[256]{0:T(256)}, ...), condition=%wide.region_1.0_spmd.clone, body=%wide.region_0.0_spmd.clone.sunk | while | flops 805896448 | bytes 5244843 | solution.py:70
  2.8 0.8 dynamic_slice.13
  3.5 0.7 add_compare_fusion.2
  4.2 4.3 %convolution_add_fusion.2 = f32[2048,256]{1,0:T(8,128)} fusion(f32[2048,256]{1,0:T(8,128)} %get-tuple-element.175, f32[256,2048]{1,0:T(8,128)} %get-tuple-element.187, s32[]{:T(128)S(6)} %select_n.20, s32[128]{0:T(128)S(1)} %dynamic_slice.13, pred[128]{0:T(512)(128)(4,1)S(1)} %add_compare_fusion.2), kind=kOutput, calls=%fused_computation.1.clone.1 | convolution fusion | flops 805896192 | bytes 5243524 | tf_op jit(solution)/shard_map/while/body/dot_general | solution.py:62
  8.4 0.8 dynamic_slice.13
  9.2 0.7 add_compare_fusion.2
  9.8 4.3 %convolution_add_fusion.2 = f32[2048,256]{1,0:T(8,128)} fusion(f32[2048,256]{1,0:T(8,128)} %get-tuple-element.175, f32[256,2048]{1,0:T(8,128)} %get-tuple-element.187, s32[]{:T(128)S(6)} %select_n.20, s32[128]{0:T(128)S(1)} %dynamic_slice.13, pred[128]{0:T(512)(128)(4,1)S(1)} %add_compare_fusion.2), kind=kOutput, calls=%fused_computation.1.clone.1 | convolution fusion | flops 805896192 | bytes 5243524 | tf_op jit(solution)/shard_map/while/body/dot_general | solution.py:62
  14.1 4.5 %all-to-all-start = ((f32[8,256,256]{2,1,0:T(8,128)}), f32[8,256,256]{2,1,0:T(8,128)S(1)}, u32[]{:S(2)}, u32[]{:S(2)}) async-start(f32[8,256,256]{2,1,0:T(8,128)} %bitcast.3), calls=%async_computation | async-start | bytes 4194304 | tf_op jit(solution)/shard_map/all_to_all | solution.py:74
  19.6 0.7 fusion.32
  20.2 0.7 slice_divide_fusion.3
  20.9 1.9 %reduce_sum.37 = f32[256]{0:T(256)S(1)} reduce(f32[2048,256]{1,0:T(8,128)} %get-tuple-element.88, f32[]{:T(128)} %constant.148.clone.1), dimensions={0}, to_apply=%region_3.0 | reduce | flops 524032 | bytes 2098180 | tf_op jit(solution)/shard_map/reduce_sum | solution.py:73
  22.9 0.6 slice.104
  23.6 0.7 fusion.31
  24.3 0.7 slice_divide_fusion.2
  25.8 0.7 fusion.30
  26.5 0.7 slice_divide_fusion.1
  28.0 0.7 fusion.29
  28.7 0.7 slice_divide_fusion
  29.5 58.6 %psum.7 = f32[256]{0:T(256)S(1)} all-reduce(f32[256]{0:T(256)S(1)} %reduce_sum.37), channel_id=1, replica_groups=mesh['cells'=8,'genes'=4] {'cells','genes'}, use_global_device_ids=true, to_apply=%region_4.5 | all-reduce | flops 256 | bytes 2048 | tf_op jit(solution)/shard_map/psum | solution.py:73
  88.1 2.5 %fusion.12 = f32[4,4096]{1,0:T(4,128)S(1)} fusion(bf16[1,1,256,4096]{3,2,1,0:T(8,128)(2,1)} %param.21, f32[256,2]{0,1:T(2,128)S(1)} %copy-done, f32[256,1]{0,1:T(1,128)S(1)} %bitcast.34, f32[4]{0:T(128)S(1)} %pad.10.clone), kind=kOutput, calls=%fused_computation.18 | convolution fusion | flops 50333696 | bytes 2165776 | tf_op jit(solution)/shard_map/dot_general | solution.py:84
  91.0 6.8 %multiply_reduce_fusion = (f32[4096]{0:T(1024)S(1)}, f32[256,4096]{1,0:T(8,128)}) fusion(f32[4,4096]{1,0:T(4,128)S(1)} %fusion.19, f32[256,2]{0,1:T(2,128)S(1)} %copy-done, f32[256,1]{0,1:T(1,128)S(1)} %bitcast.35, f32[4]{0:T(128)S(1)} %pad.10.clone, bf16[1,1,256,4096]{3,2,1,0:T(8,128)(2,1)} %param.21), kind=kOutput, calls=%fused_computation.14 | convolution fusion | flops 54523904 | bytes 6376464 | tf_op jit(solution)/shard_map/dot_general | solution.py:88
  99.3 0.8 copy.13
  100.2 9.3 %fusion.9 = f32[1,256,4096]{2,1,0:T(8,128)} fusion(f32[256,4096]{1,0:T(8,128)} %get-tuple-element.123, f32[4096]{0:T(1024)S(1)} %add_rsqrt_fusion, s32[256]{0:T(256)S(1)} %add.72, s32[256]{0:T(256)S(1)} %bitcast.39, f32[256,256]{0,1:T(8,128)S(1)} %get-tuple-element.125, f32[256]{0:T(256)S(1)} %add_rsqrt_fusion.1), kind=kOutput, calls=%fused_computation.12 | convolution fusion | flops 3227582464 | bytes 8670208 | tf_op jit(solution)/shard_map/dot_general | solution.py:95
  (40 shorter events, 5.0 us)
Async XLA Ops:
  14.1 4.5 %copy-start.3 = (s32[256]{0:T(256)S(1)}, s32[256]{0:T(256)}, u32[]{:S(2)}) copy-start(s32[256]{0:T(256)} %param.23) | copy-start | bytes 3076
  14.1 4.5 %copy-start = (f32[256,2]{0,1:T(2,128)S(1)}, f32[256,2]{0,1:T(2,128)}, u32[]{:S(2)}) copy-start(f32[256,2]{0,1:T(2,128)} %param.22) | copy-start | bytes 6148
  14.1 13.7 %copy-start.1 = (s32[1,256]{1,0:T(1,128)S(1)}, s32[1,256]{1,0:T(1,128)}, u32[]{:S(2)}) copy-start(s32[1,256]{1,0:T(1,128)} %param.24) | copy-start | bytes 3076
  14.1 13.7 %copy-start.2 = (s32[1,256]{1,0:T(1,128)S(1)}, s32[1,256]{1,0:T(1,128)}, u32[]{:S(2)}) copy-start(s32[1,256]{1,0:T(1,128)} %param.25) | copy-start | bytes 3076
  14.1 83.6 %all-to-all-start = ((f32[8,256,256]{2,1,0:T(8,128)}), f32[8,256,256]{2,1,0:T(8,128)S(1)}, u32[]{:S(2)}, u32[]{:S(2)}) async-start(f32[8,256,256]{2,1,0:T(8,128)} %bitcast.3), calls=%async_computation | async-start | bytes 4194304 | tf_op jit(solution)/shard_map/all_to_all | solution.py:74
where the time goes:
time: 110 us; the launch traced here: 109 us
  blocking collectives  58.6 us (53%)
  matrix products  28.9 us (26%)
  other arithmetic  8.95 us (8%)
  local copies, waits for them, and re-layouts  7.03 us (6%)
  starting transfers between devices  4.47 us (4%)
  between operations  1.47 us (1%)
    psum x1, blocking collectives, body(): totals = lax.psum(jnp.sum(partial_value, axis=0), ('cells', 'genes'))  58.6 us
    dot_general x1, matrix products, body(): jnp.dot(zscore_rows, dosage_z, precision=HIGHEST, preferred_element_type=...  9.29 us
    dot_general x2, matrix products, gene_major(): lax.dot_general(cell_rows, onehot, (((0,), (1,)), ((), ())), precision=HI...  8.55 us
    dot_general x1, matrix products, body(): jnp.dot(design, coef_x, precision=HIGHEST, preferred_element_type=jnp.flo...  6.76 us
    all_to_all x1, starting transfers between devices, body(): lax.all_to_all(partial_value, 'cells', split_axis=0, concat_axis=0, tiled...  4.47 us
    div x4, other arithmetic, invert(): pivot_row = augmented[pivot] / augmented[pivot, pivot]  2.61 us
    mul x4, other arithmetic, invert(): augmented = augmented - augmented[:, pivot][:, None] * pivot_row[None, :]  2.6 us
    dot_general x1, matrix products, body(): jnp.dot(design.T, dosage, precision=HIGHEST, preferred_element_type=jnp.f...  2.55 us
  transfers between devices with their start and end apart: 1, of which 0 were waited for; matrix products, arithmetic and copies ran while one was open for 19% of the time, Pallas kernels for 0%

commit v1 on v0

--- a/solution.py
+++ b/solution.py
@@ -6,6 +6,7 @@
 HIGHEST = lax.Precision.HIGHEST
 epsilon = 1e-06
 cpm_scale = 10000.0
+ports_point = lambda v0, link_axis, chip_axis: jax.lax.psum(jax.lax.psum(v0, link_axis), chip_axis)
 
 
 def design_matrix(covariates, donor_cells):
@@ -70,7 +71,7 @@
     partial_value = lax.fori_loop(
         0, block_count, gene_major, jnp.zeros((local_genes, donors), jnp.float32)
     )
-    totals = lax.psum(jnp.sum(partial_value, axis=0), ("cells", "genes"))
+    totals = ports_point(jnp.sum(partial_value, axis=0), "genes", "cells")
     pieces = lax.all_to_all(partial_value, "cells", split_axis=0, concat_axis=0, tiled=True)
     sums_rows = jnp.sum(pieces.reshape(cells_count, block_genes, donors), axis=0)
     level_rows = jnp.log1p(cpm_scale * sums_rows / (totals[None, :] + 1.0))

time: 110 us -> 96.5 us (0.88)
  the two profiles are of different devices: /device:TPU:0 before, /device:TPU:12 now
where the time goes in v1:
time: 96.5 us; the launch traced here: 96 us
  blocking collectives  45.5 us (47%)
  matrix products  28.9 us (30%)
  other arithmetic  8.96 us (9%)
  local copies, waits for them, and re-layouts  7.03 us (7%)
  starting transfers between devices  4.11 us (4%)
  between operations  1.46 us (2%)
    psum x1, blocking collectives, jax.lax.psum(jax.lax.psum(v0, link_axis), chip_axis)  39.5 us
    dot_general x1, matrix products, body(): jnp.dot(zscore_rows, dosage_z, precision=HIGHEST, preferred_element_type=...  9.3 us
    dot_general x2, matrix products, gene_major(): lax.dot_general(cell_rows, onehot, (((0,), (1,)), ((), ())), precision=HI...  8.55 us
    dot_general x1, matrix products, body(): jnp.dot(design, coef_x, precision=HIGHEST, preferred_element_type=jnp.flo...  6.76 us
    psum x1, blocking collectives, jax.lax.psum(v0, link_axis)  5.95 us
    all_to_all x1, starting transfers between devices, body(): lax.all_to_all(partial_value, 'cells', split_axis=0, concat_axis=0, tiled...  4.11 us
    div x4, other arithmetic, invert(): pivot_row = augmented[pivot] / augmented[pivot, pivot]  2.61 us
    mul x4, other arithmetic, invert(): augmented = augmented - augmented[:, pivot][:, None] * pivot_row[None, :]  2.6 us
  transfers between devices with their start and end apart: 1, of which 0 were waited for; matrix products, arithmetic and copies ran while one was open for 21% of the time, Pallas kernels for 0%

profile of v1, /device:TPU:12, one launch (start us, length us, event | category | flops | bytes accessed | tf_op | source)
XLA Modules:
  0.0 96.0 jit_solution(6833687939694063432)
XLA Ops:
  1.3 1.5 %broadcast_in_dim.16 = f32[2048,256]{1,0:T(8,128)} broadcast(f32[]{:T(128)} %constant.148.clone.1), dimensions={} | broadcast | bytes 2097156 | tf_op jit(solution)/shard_map/broadcast_in_dim | solution.py:72
  2.8 11.4 %while.15 = (s32[]{:T(128)}, f32[2048,256]{1,0:T(8,128)}, s32[]{:T(128)}, f32[256,2048]{1,0:T(8,128)}, s32[256]{0:T(256)}, /*index=5*/s32[1]{0:T(128)}, s32[]{:T(128)}, s32[]{:T(128)}, s32[]{:T(128)}, s32[]{:T(128)}) while((s32[]{:T(128)}, f32[2048,256]{1,0:T(8,128)}, s32[]{:T(128)}, f32[256,2048]{1,0:T(8,128)}, s32[256]{0:T(256)}, ...), condition=%wide.region_1.0_spmd.clone, body=%wide.region_0.0_spmd.clone.sunk | while | flops 805896448 | bytes 5244843 | solution.py:71
  2.8 0.8 dynamic_slice.13
  3.5 0.7 add_compare_fusion.2
  4.2 4.3 %convolution_add_fusion.2 = f32[2048,256]{1,0:T(8,128)} fusion(f32[2048,256]{1,0:T(8,128)} %get-tuple-element.175, f32[256,2048]{1,0:T(8,128)} %get-tuple-element.187, s32[]{:T(128)S(6)} %select_n.20, s32[128]{0:T(128)S(1)} %dynamic_slice.13, pred[128]{0:T(512)(128)(4,1)S(1)} %add_compare_fusion.2), kind=kOutput, calls=%fused_computation.1.clone.1 | convolution fusion | flops 805896192 | bytes 5243524 | tf_op jit(solution)/shard_map/while/body/dot_general | solution.py:63
  8.4 0.8 dynamic_slice.13
  9.2 0.7 add_compare_fusion.2
  9.8 4.3 %convolution_add_fusion.2 = f32[2048,256]{1,0:T(8,128)} fusion(f32[2048,256]{1,0:T(8,128)} %get-tuple-element.175, f32[256,2048]{1,0:T(8,128)} %get-tuple-element.187, s32[]{:T(128)S(6)} %select_n.20, s32[128]{0:T(128)S(1)} %dynamic_slice.13, pred[128]{0:T(512)(128)(4,1)S(1)} %add_compare_fusion.2), kind=kOutput, calls=%fused_computation.1.clone.1 | convolution fusion | flops 805896192 | bytes 5243524 | tf_op jit(solution)/shard_map/while/body/dot_general | solution.py:63
  14.1 4.1 %all-to-all-start = ((f32[8,256,256]{2,1,0:T(8,128)}), f32[8,256,256]{2,1,0:T(8,128)S(1)}, u32[]{:S(2)}, u32[]{:S(2)}) async-start(f32[8,256,256]{2,1,0:T(8,128)} %bitcast.3), calls=%async_computation | async-start | bytes 4194304 | tf_op jit(solution)/shard_map/all_to_all | solution.py:75
  19.2 0.7 fusion.32
  19.9 0.7 slice_divide_fusion.3
  20.5 1.9 %reduce_sum.37 = f32[256]{0:T(256)S(1)} reduce(f32[2048,256]{1,0:T(8,128)} %get-tuple-element.88, f32[]{:T(128)} %constant.148.clone.1), dimensions={0}, to_apply=%region_3.0 | reduce | flops 524032 | bytes 2098180 | tf_op jit(solution)/shard_map/reduce_sum | solution.py:74
  23.3 0.7 fusion.31
  23.9 0.7 slice_divide_fusion.2
  25.5 0.7 fusion.30
  26.1 0.7 slice_divide_fusion.1
  27.7 0.7 fusion.29
  28.3 0.7 slice_divide_fusion
  29.1 6.0 %psum.14 = f32[256]{0:T(256)S(1)} all-reduce(f32[256]{0:T(256)S(1)} %reduce_sum.37), channel_id=1, replica_groups=mesh['cells'=8,'genes'=4] {'genes'}, use_global_device_ids=true, to_apply=%region_4.5 | all-reduce | flops 256 | bytes 2048 | tf_op jit(solution)/shard_map/psum | solution.py:9
  35.0 39.5 %psum.15 = f32[256]{0:T(256)S(1)} all-reduce(f32[256]{0:T(256)S(1)} %psum.14), channel_id=1, replica_groups=mesh['cells'=8,'genes'=4] {'cells'}, use_global_device_ids=true, to_apply=%region_5.6 | all-reduce | flops 256 | bytes 2048 | tf_op jit(solution)/shard_map/psum | solution.py:9
  74.6 2.5 %fusion.12 = f32[4,4096]{1,0:T(4,128)S(1)} fusion(bf16[1,1,256,4096]{3,2,1,0:T(8,128)(2,1)} %param.21, f32[256,2]{0,1:T(2,128)S(1)} %copy-done, f32[256,1]{0,1:T(1,128)S(1)} %bitcast.34, f32[4]{0:T(128)S(1)} %pad.10.clone), kind=kOutput, calls=%fused_computation.18 | convolution fusion | flops 50333696 | bytes 2165776 | tf_op jit(solution)/shard_map/dot_general | solution.py:85
  77.5 6.8 %multiply_reduce_fusion = (f32[4096]{0:T(1024)S(1)}, f32[256,4096]{1,0:T(8,128)}) fusion(f32[4,4096]{1,0:T(4,128)S(1)} %fusion.19, f32[256,2]{0,1:T(2,128)S(1)} %copy-done, f32[256,1]{0,1:T(1,128)S(1)} %bitcast.35, f32[4]{0:T(128)S(1)} %pad.10.clone, bf16[1,1,256,4096]{3,2,1,0:T(8,128)(2,1)} %param.21), kind=kOutput, calls=%fused_computation.14 | convolution fusion | flops 54523904 | bytes 6376464 | tf_op jit(solution)/shard_map/dot_general | solution.py:89
  85.8 0.8 copy.13
  86.7 9.3 %fusion.9 = f32[1,256,4096]{2,1,0:T(8,128)} fusion(f32[256,4096]{1,0:T(8,128)} %get-tuple-element.123, f32[4096]{0:T(1024)S(1)} %add_rsqrt_fusion, s32[256]{0:T(256)S(1)} %add.74, s32[256]{0:T(256)S(1)} %bitcast.39, f32[256,256]{0,1:T(8,128)S(1)} %get-tuple-element.125, f32[256]{0:T(256)S(1)} %add_rsqrt_fusion.1), kind=kOutput, calls=%fused_computation.12 | convolution fusion | flops 3227582464 | bytes 8670208 | tf_op jit(solution)/shard_map/dot_general | solution.py:96
  (41 shorter events, 5.6 us)
Async XLA Ops:
  14.1 4.1 %copy-start.3 = (s32[256]{0:T(256)S(1)}, s32[256]{0:T(256)}, u32[]{:S(2)}) copy-start(s32[256]{0:T(256)} %param.23) | copy-start | bytes 3076
  14.1 4.2 %copy-start = (f32[256,2]{0,1:T(2,128)S(1)}, f32[256,2]{0,1:T(2,128)}, u32[]{:S(2)}) copy-start(f32[256,2]{0,1:T(2,128)} %param.22) | copy-start | bytes 6148
  14.1 13.4 %copy-start.1 = (s32[1,256]{1,0:T(1,128)S(1)}, s32[1,256]{1,0:T(1,128)}, u32[]{:S(2)}) copy-start(s32[1,256]{1,0:T(1,128)} %param.24) | copy-start | bytes 3076
  14.1 13.4 %copy-start.2 = (s32[1,256]{1,0:T(1,128)S(1)}, s32[1,256]{1,0:T(1,128)}, u32[]{:S(2)}) copy-start(s32[1,256]{1,0:T(1,128)} %param.25) | copy-start | bytes 3076
  14.1 70.1 %all-to-all-start = ((f32[8,256,256]{2,1,0:T(8,128)}), f32[8,256,256]{2,1,0:T(8,128)S(1)}, u32[]{:S(2)}, u32[]{:S(2)}) async-start(f32[8,256,256]{2,1,0:T(8,128)} %bitcast.3), calls=%async_computation | async-start | bytes 4194304 | tf_op jit(solution)/shard_map/all_to_all | solution.py:75
